TPU v7x, 32 devices: a whole 2x2x4 slice. The times are simulated.
32 devices in a mesh: dp: 4 (over y, x), expert: 8 (over z, core).
Axes of the slice: x: 2, y: 2, z: 4, core: 2. Of those that a mesh axis runs over, the one named last changes fastest.
Arguments:
- tokens: bfloat16 [8192, 2048], P(('dp', 'expert')), may hold values from -6 to 6
- expert_ids: int32 [8192, 8], P(('dp', 'expert')), may hold values from 0 to 15, all different within a row; in each aligned block of 256 rows (0 to 255, 256 to 511, ...) at most 160 rows name the same one
- route_probs: float32 [8192, 8], P(('dp', 'expert')), may hold values from 0.05 to 1
- w_gate_up: bfloat16 [16, 2048, 1536], P('expert', 'dp'), may hold values from -0.125 to 0.125
- w_down: bfloat16 [16, 768, 2048], P('expert', None, 'dp'), may hold values from -0.21875 to 0.21875
Outputs:
- moe_out: bfloat16 [8192, 2048], P(('dp', 'expert'))
Inputs may be any that keep to these rules, and one draw needn't show every extreme that they name: `expert_ids`: each row names 8 different experts. Among the rows of one device no expert is named more than 160 times, and in every draw some expert is named exactly 160 times in some device's rows.
All inputs are finite; a program needn't handle non-finite values.
Results may differ from a plain program's by a relative error of at most 0.0057.
Values may be sent and summed in bfloat16 or wider, within the bound.
A program may use at most 128 MiB of HBM per device.

v0:
```python
import functools

import jax
import jax.numpy as jnp
from jax import lax
from jax.experimental import pallas as pl
from jax.experimental.pallas import tpu as pltpu
from jax.sharding import PartitionSpec as P

MESH = pl.DeviceIdType.MESH


def xor(index, mask):
    width = 1
    while width <= mask:
        if mask & width:
            index = index + width * (1 - 2 * lax.rem(index // width, 2))
        width *= 2
    return index


def span(masks):
    out = [0]
    for m in masks:
        out = out + [m ^ s for s in out]
    return out


class Gather:
    def __init__(self, orders, me, target, own, slot, send_sem, recv_sem):
        self.orders, self.me, self.target = orders, me, target
        self.own, self.slot = own, slot
        self.send_sem, self.recv_sem = send_sem, recv_sem
        self.started = []

    def stages(self):
        return len(self.orders[0])

    def send(self, stage):
        for half, order in enumerate(self.orders):
            g = order[stage]
            for s in span(order[:stage]):
                block = xor(self.me, s)
                dst = self.slot(block, half)
                copy = pltpu.make_async_remote_copy(
                    src_ref=self.own(half) if s == 0 else dst,
                    dst_ref=dst,
                    send_sem=self.send_sem.at[half, g ^ s],
                    recv_sem=self.recv_sem.at[half, g ^ s],
                    device_id=self.target(xor(self.me, g)),
                    device_id_type=MESH,
                )
                copy.start()
                self.started.append(copy)

    def wait(self, stage):
        for half, order in enumerate(self.orders):
            g = order[stage]
            for s in span(order[:stage]):
                ref = self.slot(xor(self.me, g ^ s), half)
                pltpu.make_async_remote_copy(
                    src_ref=ref,
                    dst_ref=ref,
                    send_sem=self.send_sem.at[half, g ^ s],
                    recv_sem=self.recv_sem.at[half, g ^ s],
                    device_id=self.target(xor(self.me, g)),
                    device_id_type=MESH,
                ).wait_recv()

    def drain(self):
        for copy in self.started:
            copy.wait_send()


def powers(count):
    out, width = [], 1
    while width < count:
        out.append(width)
        width *= 2
    return out


def kernel(
    dps, owners,
    tok_in, share_in, gu_in, dn_in, got,
    tok, share, gu, dn, hid, sib, near,
    tok_s, tok_r, share_s, share_r, gu_s, gu_r, dn_s, dn_r, sib_s, sib_r, near_s, near_r, out_s, out_r, loc,
):
    dp, ex = lax.axis_index("dp"), lax.axis_index("expert")
    chips, pairs = owners // 2, owners // 4
    chip, core = ex // 2, lax.rem(ex, 2)
    pair, side = chip // 2, lax.rem(chip, 2)
    local = gu_in.shape[0]
    depth = gu_in.shape[1]
    cols = dn_in.shape[2]
    rows, width = tok_in.shape
    ff = dn_in.shape[1]

    dp_masks = powers(dps)
    chip_masks = [2 * (2 * w - 1) for w in powers(chips)]

    barrier = pltpu.get_barrier_semaphore()
    peers = [(xor(dp, m), ex) for m in dp_masks] + [(dp, xor(ex, r)) for r in range(1, owners)]
    for peer in peers:
        pl.semaphore_signal(barrier, inc=1, device_id=peer, device_id_type=MESH)
    pl.semaphore_wait(barrier, len(peers))

    def on_expert(index):
        return (dp, index)

    def on_dp(index):
        return (index, ex)

    half_rows, half_depth, half_ff = rows // 2, depth // 2, ff // 2
    tokens = Gather(
        [chip_masks + [1], chip_masks[::-1] + [1]], ex, on_expert,
        lambda h: tok_in.at[pl.ds(h * half_rows, half_rows)],
        lambda b, h: tok.at[b // 4, lax.rem(b // 2, 2), lax.rem(b, 2), pl.ds(h * half_rows, half_rows)],
        tok_s, tok_r,
    )
    ups = [
        Gather(
            [dp_masks, dp_masks[::-1]], dp, on_dp,
            lambda h, e=e: gu_in.at[e, pl.ds(h * half_depth, half_depth)],
            lambda b, h, e=e: gu.at[e, pl.ds(pl.multiple_of(b * depth + h * half_depth, half_depth), half_depth)],
            gu_s.at[e], gu_r.at[e],
        )
        for e in range(local)
    ]
    down = Gather(
        [dp_masks, dp_masks[::-1]], dp, on_dp,
        lambda h: dn_in.at[:, pl.ds(h * half_ff, half_ff)],
        lambda b, h: dn.at[b, :, pl.ds(h * half_ff, half_ff)],
        dn_s, dn_r,
    )

    tokens.send(0)
    for e in range(local):
        ups[e].send(0)
    shares = []
    for r in range(1, owners):
        copy = pltpu.make_async_remote_copy(
            src_ref=share_in.at[xor(ex, r)], dst_ref=share.at[ex],
            send_sem=share_s.at[r], recv_sem=share_r.at[r],
            device_id=(dp, xor(ex, r)), device_id_type=MESH,
        )
        copy.start()
        shares.append(copy)
    locals_ = [
        pltpu.make_async_copy(tok_in, tok.at[pair, side, core], loc.at[0]),
        pltpu.make_async_copy(share_in.at[ex], share.at[ex], loc.at[1]),
        pltpu.make_async_copy(
            gu_in, gu.at[:, pl.ds(pl.multiple_of(dp * depth, depth), depth)], loc.at[2]
        ),
        pltpu.make_async_copy(dn_in, dn.at[dp], loc.at[3]),
    ]
    for copy in locals_:
        copy.start()

    last = len(dp_masks) - 1
    queue = [(g, stage) for g in ups for stage in range(1, last + 1)]
    tok_stage, tok_last = 0, tokens.stages() - 1

    def step_tokens():
        nonlocal tok_stage
        if tok_stage < tok_last:
            tokens.wait(tok_stage)
            tok_stage += 1
            tokens.send(tok_stage)

    for at, (g, stage) in enumerate(queue):
        step_tokens()
        g.wait(stage - 1)
        g.send(stage)
    down.send(0)
    while tok_stage < tok_last:
        step_tokens()
    tokens.wait(tok_last)
    for copy in locals_:
        copy.wait()

    tile = 256 if ff % 256 == 0 else ff

    def hidden(e):
        def body(c, carry):
            x = tok[c // 2, lax.rem(c, 2)].reshape(2 * rows, width)
            for f in range(ff // tile):
                a = jnp.dot(x, gu[e, :, f * tile:(f + 1) * tile], preferred_element_type=jnp.float32)
                b = jnp.dot(
                    x, gu[e, :, ff + f * tile:ff + (f + 1) * tile], preferred_element_type=jnp.float32
                )
                hid[e, c, :, f * tile:(f + 1) * tile] = (a / (1.0 + jnp.exp(-a)) * b).astype(hid.dtype)
            return carry

        lax.fori_loop(0, chips, body, 0)

    for e in range(local):
        ups[e].wait(last)
        hidden(e)
        if e == 0:
            for stage in range(1, last + 1):
                down.wait(stage - 1)
                down.send(stage)

    tokens.drain()
    for r, copy in enumerate(shares):
        pltpu.make_async_remote_copy(
            src_ref=share_in.at[0], dst_ref=share.at[xor(ex, r + 1)],
            send_sem=share_s.at[r + 1], recv_sem=share_r.at[r + 1],
            device_id=(dp, xor(ex, r + 1)), device_id_type=MESH,
        ).wait_recv()

    def partial(b):
        at = pl.ds(pl.multiple_of(b * cols, cols), cols)

        def body(c, carry):
            parts = [
                jnp.dot(hid[e, c], dn[b, e], preferred_element_type=jnp.float32) for e in range(local)
            ]
            for k in range(2):
                scale = jnp.transpose(share[2 * c + k])
                total = parts[0][k * rows:(k + 1) * rows] * scale[:, 0:1]
                for e in range(1, local):
                    total = total + parts[e][k * rows:(k + 1) * rows] * scale[:, e:e + 1]
                tok[c // 2, lax.rem(c, 2), k, :, at] = total.astype(tok.dtype)
            return carry

        lax.fori_loop(0, chips, body, 0)

    def to_sibling(s, b):
        at = pl.ds(pl.multiple_of(b * cols, cols), cols)
        copy = pltpu.make_async_remote_copy(
            src_ref=tok.at[:, :, 1 - core, :, at], dst_ref=sib.at[:, :, :, at],
            send_sem=sib_s.at[s], recv_sem=sib_r.at[s],
            device_id=(dp, xor(ex, 1)), device_id_type=MESH,
        )
        return copy

    def add(c, side_, ref, at):
        tok[c, side_, core, :, at] = (
            tok[c, side_, core, :, at].astype(jnp.float32) + ref[...].astype(jnp.float32)
        ).astype(tok.dtype)

    def to_near(s, b):
        at = pl.ds(pl.multiple_of(b * cols, cols), cols)

        def body(c, carry):
            add(c, 1 - side, sib.at[c, 1 - side, :, at], at)
            return carry

        lax.fori_loop(0, pairs, body, 0)

        def body_own(c, carry):
            add(c, side, sib.at[c, side, :, at], at)
            return carry

        lax.fori_loop(0, pairs, body_own, 0)
        return pltpu.make_async_remote_copy(
            src_ref=tok.at[:, 1 - side, core, :, at], dst_ref=near.at[:, :, at],
            send_sem=near_s.at[s], recv_sem=near_r.at[s],
            device_id=(dp, xor(ex, 2)), device_id_type=MESH,
        )

    sent = []

    def home(s, b):
        at = pl.ds(pl.multiple_of(b * cols, cols), cols)

        def body(c, carry):
            add(c, side, near.at[c, :, at], at)
            return carry

        lax.fori_loop(0, pairs, body, 0)
        for r in range(1, pairs):
            copy = pltpu.make_async_remote_copy(
                src_ref=tok.at[xor(pair, r), side, core, :, at], dst_ref=got.at[pair, :, at],
                send_sem=out_s.at[s, r], recv_sem=out_r.at[s, r],
                device_id=(dp, xor(ex, 4 * r)), device_id_type=MESH,
            )
            copy.start()
            sent.append(copy)
        own = pltpu.make_async_copy(tok.at[pair, side, core, :, at], got.at[pair, :, at], out_r.at[s, 0])
        own.start()
        sent.append(own)

    first, second = {}, {}
    for s in range(dps + 2):
        if s < dps:
            if s == 1:
                down.wait(last)
            partial(xor(dp, s))
            first[s] = to_sibling(s, xor(dp, s))
            first[s].start()
        if 1 <= s < dps + 1:
            first[s - 1].wait()
            second[s - 1] = to_near(s - 1, xor(dp, s - 1))
            second[s - 1].start()
        if s >= 2:
            second[s - 2].wait()
            home(s - 2, xor(dp, s - 2))

    for s in range(dps):
        b = xor(dp, s)
        at = pl.ds(pl.multiple_of(b * cols, cols), cols)
        for r in range(1, pairs):
            pltpu.make_async_remote_copy(
                src_ref=tok.at[pair, side, core, :, at], dst_ref=got.at[xor(pair, r), :, at],
                send_sem=out_s.at[s, r], recv_sem=out_r.at[s, r],
                device_id=(dp, xor(ex, 4 * r)), device_id_type=MESH,
            ).wait_recv()
    for at, copy in enumerate(sent):
        if at % pairs == pairs - 1:
            copy.wait()
        else:
            copy.wait_send()
    for copy in shares:
        copy.wait_send()
    for g in ups + [down]:
        g.drain()


def shards(tokens, expert_ids, route_probs, w_gate_up, w_down):
    dps, owners = lax.axis_size("dp"), lax.axis_size("expert")
    chips, pairs = owners // 2, owners // 4
    local, depth, both = w_gate_up.shape
    experts = owners * local
    rows, width = tokens.shape
    ff, cols = w_down.shape[1:]
    weights = route_probs / jnp.sum(route_probs, axis=1, keepdims=True)
    share = jnp.sum(
        jnp.where(
            expert_ids.T[None] == jnp.arange(experts, dtype=jnp.int32)[:, None, None],
            weights.T[None], 0.0,
        ),
        axis=1,
    ).reshape(owners, local, rows)
    pad = -local % 8
    share = jnp.pad(share, ((0, 0), (0, pad), (0, 0)))
    any_ = pl.BlockSpec(memory_space=pl.ANY)
    dma = pltpu.SemaphoreType.DMA
    bf16 = jnp.bfloat16
    got = pl.pallas_call(
        functools.partial(kernel, dps, owners),
        out_shape=jax.ShapeDtypeStruct((pairs, rows, width), bf16),
        in_specs=[any_] * 4,
        out_specs=any_,
        scratch_shapes=[
            pltpu.VMEM((pairs, 2, 2, rows, width), bf16),
            pltpu.VMEM((owners, local + pad, rows), jnp.float32),
            pltpu.VMEM((local, dps * depth, both), bf16),
            pltpu.VMEM((dps, local, ff, cols), bf16),
            pltpu.VMEM((local, chips, 2 * rows, ff), bf16),
            pltpu.VMEM((pairs, 2, rows, width), bf16),
            pltpu.VMEM((pairs, rows, width), bf16),
            dma((2, owners)), dma((2, owners)),
            dma((owners,)), dma((owners,)),
            dma((local, 2, dps)), dma((local, 2, dps)),
            dma((2, dps)), dma((2, dps)),
            dma((dps,)), dma((dps,)),
            dma((dps,)), dma((dps,)),
            dma((dps, pairs)), dma((dps, pairs)),
            dma((4,)),
        ],
        compiler_params=pltpu.CompilerParams(
            collective_id=0, has_side_effects=True, vmem_limit_bytes=67043328
        ),
    )(tokens, share, w_gate_up, w_down)
    return jnp.sum(got.astype(jnp.float32), axis=0).astype(bf16)


def solution(mesh):
    return jax.shard_map(
        shards,
        mesh=mesh,
        in_specs=(
            P(("dp", "expert"), None),
            P(("dp", "expert"), None),
            P(("dp", "expert"), None),
            P("expert", "dp", None),
            P("expert", None, "dp"),
        ),
        out_specs=P(("dp", "expert"), None),
        check_vma=False,
    )
```

profile of v0, /device:TPU:0, one launch (start us, length us, event | category | flops | bytes accessed | tf_op | source)
XLA Modules:
  0.0 249.6 jit_solution(6223632030234905862)
XLA Ops:
  0.0 0.7 reduce_sum.30
  0.7 0.7 divide_bitcast_fusion
  1.4 0.7 select_reduce_fusion
  2.2 0.6 pad.4.share_in
  2.8 243.5 %shard_map.55 = bf16[2,256,2048]{2,1,0:T(8,128)(2,1)} custom-call(bf16[256,2048]{1,0:T(8,128)(2,1)} %tok_in.1, f32[8,8,256]{2,1,0:T(8,128)} %pad.4.share_in, bf16[2,512,1536]{2,1,0:T(8,128)(2,1)} %gu_in.1, bf16[2,768,512]{2,1,0:T(8,128)(2,1)} %dn_in.1), custom_call_target="tpu_custom_call" | custom-call | tf_op jit(solution)/shard_map/pallas_call | solution.py:342
  246.3 3.3 %reduce_sum.32 = bf16[256,2048]{1,0:T(8,128)(2,1)} reduce(bf16[2,256,2048]{2,1,0:T(8,128)(2,1)} %shard_map.55, bf16[]{:T(256)} %constant.5.clone.1), dimensions={0}, to_apply=%region_2.3 | reduce | flops 524288 | bytes 3145730 | tf_op jit(solution)/shard_map/reduce_sum | solution.py:368
  (1 shorter events, 0.0 us)
where the time goes:
time: 250 us
  Pallas kernels  244 us (98%)
  other arithmetic  5.47 us (2%)
    pallas_call x1, Pallas kernels, shards(): pl.pallas_call(functools.partial(kernel, dps, owners), out_shape=jax.Shap...  244 us

commit v1 on v0

v1 whole, which is shorter than its diff:
```python
import functools

import jax
import jax.numpy as jnp
from jax import lax
from jax.experimental import pallas as pl
from jax.experimental.pallas import tpu as pltpu
from jax.sharding import PartitionSpec as P

MESH = pl.DeviceIdType.MESH
LANES = 128


def xor(index, mask):
    width = 1
    while width <= mask:
        if mask & width:
            index = index + width * (1 - 2 * lax.rem(index // width, 2))
        width *= 2
    return index


def span(masks):
    out = [0]
    for m in masks:
        out = out + [m ^ s for s in out]
    return out


def powers(count):
    out, width = [], 1
    while width < count:
        out.append(width)
        width *= 2
    return out


class Gather:
    def __init__(self, orders, me, target, own, slot, send_sem, recv_sem):
        self.orders, self.me, self.target = orders, me, target
        self.own_ref, self.slot = own, slot
        self.send_sem, self.recv_sem = send_sem, recv_sem
        self.last = len(orders[0]) - 1
        self.taken = set()

    def _copy(self, half, g, s):
        dst = self.slot(xor(self.me, s), half)
        return pltpu.make_async_remote_copy(
            src_ref=self.own_ref(half) if s == 0 else dst,
            dst_ref=dst,
            send_sem=self.send_sem.at[half, g ^ s],
            recv_sem=self.recv_sem.at[half, g ^ s],
            device_id=self.target(xor(self.me, g)),
            device_id_type=MESH,
        )

    def own(self, stage):
        for half, order in enumerate(self.orders):
            self._copy(half, order[stage], 0).start()

    def relay(self, stage):
        for half, order in enumerate(self.orders):
            for s in span(order[:stage])[1:]:
                self._copy(half, order[stage], s).start()

    def take(self, half, off):
        if (half, off) in self.taken:
            return
        self.taken.add((half, off))
        ref = self.slot(xor(self.me, off), half)
        pltpu.make_async_remote_copy(
            src_ref=ref,
            dst_ref=ref,
            send_sem=self.send_sem.at[half, off],
            recv_sem=self.recv_sem.at[half, off],
            device_id=self.target(xor(self.me, off)),
            device_id_type=MESH,
        ).wait_recv()

    def wait(self, stage):
        for half, order in enumerate(self.orders):
            for s in span(order[:stage]):
                self.take(half, order[stage] ^ s)

    def forward(self):
        for stage in range(1, self.last + 1):
            self.wait(stage - 1)
            self.relay(stage)

    def drain(self):
        for half, order in enumerate(self.orders):
            for stage, g in enumerate(order):
                for s in span(order[:stage]):
                    self._copy(half, g, s).wait_send()


def kernel(
    dps, owners,
    tok_in, ids_in, prob_in, gu_in, dn_in, out,
    tok, share_out, share, gu, dn, hid, near, got,
    tok_s, tok_r, share_s, share_r, gu_s, gu_r, gus_s, gus_r, dn_s, dn_r, dns_s, dns_r,
    near_s, near_r, out_s, out_r, loc, gu_l, dn_l, fin,
):
    dp, ex = lax.axis_index("dp"), lax.axis_index("expert")
    chips, pairs = owners // 2, owners // 4
    chip, core = ex // 2, lax.rem(ex, 2)
    pair, side = chip // 2, lax.rem(chip, 2)
    local, depth, both = gu_in.shape
    ff, cols = dn_in.shape[1:]
    rows, width = tok_in.shape
    count = 2 * local
    tiles, strips = ff // LANES, cols // LANES
    units = local * tiles
    mine = local * ff

    dp_masks = powers(dps)
    chip_masks = [2 * (2 * w - 1) for w in powers(chips)]

    barrier = pltpu.get_barrier_semaphore()
    peers = [(xor(dp, m), ex) for m in dp_masks] + [(dp, xor(ex, 1))]
    peers += [(dp, xor(ex, 2 * r)) for r in range(1, chips)]
    for peer in peers:
        pl.semaphore_signal(barrier, inc=1, device_id=peer, device_id_type=MESH)

    def on_expert(index):
        return (dp, index)

    def on_dp(index):
        return (index, ex)

    sibling = (dp, xor(ex, 1))

    def stage_unit(u):
        e, j = u // tiles, lax.rem(u, tiles)
        at = pl.ds(pl.multiple_of(dp * depth, depth), depth)
        return [
            pltpu.make_async_copy(
                gu_in.at[e, :, pl.ds(pl.multiple_of(k * ff + j * LANES, LANES), LANES)],
                gu.at[u, at, pl.ds(k * LANES, LANES)],
                gu_l.at[u, k],
            )
            for k in range(2)
        ]

    def stage_strip(s):
        return [
            pltpu.make_async_copy(
                dn_in.at[e, :, pl.ds(s * LANES, LANES)], dn.at[s, dp, pl.ds(e * ff, ff)], dn_l.at[s, e]
            )
            for e in range(local)
        ]

    own_tok = pltpu.make_async_copy(tok_in, tok.at[pair, side], loc.at[0])

    @functools.partial(lax.fori_loop, 0, units, init_val=0)
    def _(u, carry):
        for copy in stage_unit(u):
            copy.start()
        return carry

    own_tok.start()
    for s in range(strips):
        for copy in stage_strip(s):
            copy.start()

    half_rows, half_depth, half_mine = rows // 2, depth // 2, mine // 2
    tokens = Gather(
        [chip_masks, chip_masks[::-1]], ex, on_expert,
        lambda h: tok_in.at[pl.ds(h * half_rows, half_rows)],
        lambda b, h: tok.at[b // 4, lax.rem(b // 2, 2), pl.ds(h * half_rows, half_rows)],
        tok_s, tok_r,
    )

    def up(u):
        def slot(b, h):
            return gu.at[u, pl.ds(pl.multiple_of(b * depth + h * half_depth, half_depth), half_depth)]

        return Gather(
            [dp_masks, dp_masks[::-1]], dp, on_dp, lambda h: slot(dp, h), slot, gu_s.at[u], gu_r.at[u]
        )

    def down(s):
        def slot(b, h):
            return dn.at[s, b, pl.ds(h * half_mine, half_mine)]

        return Gather(
            [dp_masks, dp_masks[::-1]], dp, on_dp, lambda h: slot(dp, h), slot, dn_s.at[s], dn_r.at[s]
        )

    last = len(dp_masks) - 1

    def up_own(u):
        for copy in stage_unit(u):
            copy.wait()
        g = up(u)
        for stage in range(last + 1):
            g.own(stage)

    def down_own(s):
        g = down(s)
        for stage in range(last + 1):
            g.own(stage)

    def up_sib(u):
        return pltpu.make_async_remote_copy(
            src_ref=gu.at[u], dst_ref=gu.at[units + u], send_sem=gus_s.at[u], recv_sem=gus_r.at[u],
            device_id=sibling, device_id_type=MESH,
        )

    def down_sib(s, b, m):
        return pltpu.make_async_remote_copy(
            src_ref=dn.at[s, b, pl.ds(0, mine)], dst_ref=dn.at[s, b, pl.ds(mine, mine)],
            send_sem=dns_s.at[s, m], recv_sem=dns_r.at[s, m],
            device_id=sibling, device_id_type=MESH,
        )

    pl.semaphore_wait(barrier, len(peers))
    for stage in range(tokens.last + 1):
        tokens.own(stage)
    up_own(0)
    up_own(1)

    prob = prob_in[...]
    weight = prob / jnp.sum(prob, axis=0, keepdims=True)
    ids = ids_in[...]
    pad = share_out.shape[1] - count
    for c in range(chips):
        lines = [
            jnp.sum(
                jnp.where(ids == c * count + lax.rem(core * local + k, count), weight, 0.0), axis=0, keepdims=True
            )
            for k in range(count)
        ]
        if pad:
            lines.append(jnp.zeros((pad, rows), jnp.float32))
        share_out[c] = jnp.concatenate(lines, axis=0)

    def to_chip(r):
        other = xor(ex, 2 * r)
        return pltpu.make_async_remote_copy(
            src_ref=share_out.at[other // 2], dst_ref=share.at[chip],
            send_sem=share_s.at[r], recv_sem=share_r.at[r],
            device_id=on_expert(other), device_id_type=MESH,
        )

    for r in range(1, chips):
        to_chip(r).start()

    fold = 2 if pairs <= 2 else 1

    def hidden(p, v):
        def body(i, carry):
            x = tok[p, pl.ds(i * fold, fold)].reshape(fold * rows, width)
            ab = jnp.dot(x, gu[v], preferred_element_type=jnp.float32)
            a, b = ab[:, :LANES], ab[:, LANES:]
            by = jnp.concatenate([jnp.transpose(share[2 * p + i * fold + k]) for k in range(fold)], axis=0)
            lane = lax.broadcasted_iota(jnp.int32, by.shape, 1)
            by = jnp.sum(jnp.where(lane == v // tiles, by, 0.0), axis=1, keepdims=True)
            at = pl.ds(pl.multiple_of(i * fold * rows, fold * rows), fold * rows)
            hid[p, at, pl.ds(pl.multiple_of(v * LANES, LANES), LANES)] = (
                a / (1.0 + jnp.exp(-a)) * b * by
            ).astype(hid.dtype)
            return carry

        if fold == 2:
            body(0, 0)
        else:
            lax.fori_loop(0, 2, body, 0)

    def relay_step(u, ahead):
        @pl.when(u + ahead < units)
        def _():
            up_own(u + ahead)

        @pl.when(u + 1 < units)
        def _():
            up(u + 1).forward()

        @pl.when(u + 2 == units)
        def _():
            down_own(0)

    begin, early = units // 3, 2 * units // 3

    up(0).forward()
    for u in range(begin):
        relay_step(u, 2)
        if u == begin // 2:
            tokens.forward()
        up(u).wait(last)
        up_sib(u).start()

    own_tok.wait()
    for half in range(2):
        tokens.take(half, 2)
    share_own = share_out[chip]
    share[chip] = share_own
    for r in range(1, chips):
        pltpu.make_async_remote_copy(
            src_ref=share_out.at[0], dst_ref=share.at[xor(ex, 2 * r) // 2],
            send_sem=share_s.at[r], recv_sem=share_r.at[r],
            device_id=on_expert(xor(ex, 2 * r)), device_id_type=MESH,
        ).wait_recv()

    def both_of(v):
        hidden(pair, v)
        up_sib(v).wait_recv()
        hidden(pair, units + v)

    def phase_one(u, carry):
        relay_step(u, 2)
        share_of(u - begin, begin, early - begin, both_of)
        up(u).wait(last)
        up_sib(u).start()
        both_of(u)
        return carry

    def share_of(i, total, parts, body):
        each = -(-total // parts)

        def one(n, carry):
            @pl.when(i * each + n < total)
            def _():
                body(i * each + n)

            return carry

        lax.fori_loop(0, each, one, 0)

    lax.fori_loop(begin, early, phase_one, 0)

    for copy in [c for s in range(strips) for c in stage_strip(s)]:
        copy.wait()
    for s in range(strips):
        down_sib(s, dp, 0).start()
    tokens.wait(tokens.last)
    for stage in range(tokens.last):
        tokens.wait(stage)

    def others_of(v):
        for r in range(1, pairs):
            hidden(xor(pair, r), v)
            hidden(xor(pair, r), units + v)

    def phase_two(u, carry):
        relay_step(u, 2)
        share_of(u - early, early, units - early, others_of)
        up(u).wait(last)
        up_sib(u).start()

        def every(p, v):
            hidden(p, v)
            return v

        lax.fori_loop(0, pairs, every, u)
        up_sib(u).wait_recv()
        lax.fori_loop(0, pairs, every, units + u)
        return carry

    lax.fori_loop(early, units, phase_two, 0)

    tokens.drain()

    steps = [(s, 0) for s in range(strips)] + [(s, m) for s in range(strips) for m in range(1, dps)]

    def where(k):
        s, m = steps[k]
        return pl.ds(pl.multiple_of(xor(dp, m) * cols + s * LANES, LANES), LANES)

    def to_near(k):
        at = where(k)
        return pltpu.make_async_remote_copy(
            src_ref=tok.at[:, 1 - side, :, at], dst_ref=near.at[:, :, at],
            send_sem=near_s.at[k], recv_sem=near_r.at[k],
            device_id=on_expert(xor(ex, 2)), device_id_type=MESH,
        )

    def to_home(k, r):
        at = where(k)
        return pltpu.make_async_remote_copy(
            src_ref=tok.at[xor(pair, r), side, :, at], dst_ref=got.at[r - 1, :, at],
            send_sem=out_s.at[k, r], recv_sem=out_r.at[k, r],
            device_id=on_expert(xor(ex, 4 * r)), device_id_type=MESH,
        )

    def to_out(k):
        at = where(k)
        return pltpu.make_async_copy(tok.at[pair, side, :, at], out.at[:, at], fin.at[k])

    def partial(k):
        s, m = steps[k]
        b, at = xor(dp, m), where(k)

        def body(p, carry):
            total = jnp.dot(hid[p], dn[s, b], preferred_element_type=jnp.float32)
            tok[p, :, :, at] = total.astype(tok.dtype).reshape(2, rows, LANES)
            return carry

        lax.fori_loop(0, pairs, body, 0)
        to_near(k).start()

    def pass_on(k):
        at = where(k)
        to_near(k).wait_recv()
        for r in range(1, pairs):
            p = xor(pair, r)
            tok[p, side, :, at] = (
                tok[p, side, :, at].astype(jnp.float32) + near[p, :, at].astype(jnp.float32)
            ).astype(tok.dtype)
            to_home(k, r).start()

    def finish(k):
        at = where(k)
        total = tok[pair, side, :, at].astype(jnp.float32) + near[pair, :, at].astype(jnp.float32)
        for r in range(1, pairs):
            to_home(k, r).wait_recv()
            total = total + got[r - 1, :, at].astype(jnp.float32)
        tok[pair, side, :, at] = total.astype(tok.dtype)
        to_out(k).start()

    lag = 2

    def advance(k):
        if k < len(steps):
            partial(k)
        if 0 <= k - lag < len(steps):
            pass_on(k - lag)
        if 0 <= k - 2 * lag < len(steps):
            finish(k - 2 * lag)

    if strips > 1:
        down_own(1)
    for s in range(strips):
        down_sib(s, dp, 0).wait_recv()
        advance(s)
        if s == 0:
            down(0).forward()
        if s == strips // 2:
            if strips > 2:
                down_own(2)
            if strips > 1:
                down(1).forward()
    k = strips
    for s in range(strips):
        down(s).wait(last)
        for m in range(1, dps):
            down_sib(s, xor(dp, m), m).start()
        for m in range(1, dps):
            down_sib(s, xor(dp, m), m).wait_recv()
            advance(k)
            k += 1
            if m == 1:
                if s + 3 < strips:
                    down_own(s + 3)
                if s + 2 < strips:
                    down(s + 2).forward()
    while k < len(steps) + 2 * lag:
        advance(k)
        k += 1

    def drained(u, carry):
        up(u).drain()
        up_sib(u).wait_send()
        return carry

    lax.fori_loop(0, units, drained, 0)
    for s in range(strips):
        down(s).drain()
        for m in range(dps):
            down_sib(s, xor(dp, m), m).wait_send()
    for r in range(1, chips):
        to_chip(r).wait_send()
    for k in range(len(steps)):
        to_near(k).wait_send()
        for r in range(1, pairs):
            to_home(k, r).wait_send()
        to_out(k).wait()


def shards(tokens, expert_ids, route_probs, w_gate_up, w_down):
    dps, owners = lax.axis_size("dp"), lax.axis_size("expert")
    chips, pairs = owners // 2, owners // 4
    local, depth, both = w_gate_up.shape
    rows, width = tokens.shape
    ff, cols = w_down.shape[1:]
    count = 2 * local
    lines = count + -count % 8
    tiles, strips = ff // LANES, cols // LANES
    units, steps = local * tiles, strips * dps
    any_ = pl.BlockSpec(memory_space=pl.ANY)
    vmem = pl.BlockSpec(memory_space=pltpu.VMEM)
    dma = pltpu.SemaphoreType.DMA
    bf16, f32 = jnp.bfloat16, jnp.float32
    return pl.pallas_call(
        functools.partial(kernel, dps, owners),
        out_shape=jax.ShapeDtypeStruct((rows, width), bf16),
        in_specs=[any_, vmem, vmem, any_, any_],
        out_specs=any_,
        scratch_shapes=[
            pltpu.VMEM((pairs, 2, rows, width), bf16),
            pltpu.VMEM((chips, lines, rows), f32),
            pltpu.VMEM((chips, lines, rows), f32),
            pltpu.VMEM((2 * units, dps * depth, 2 * LANES), bf16),
            pltpu.VMEM((strips, dps, count * ff, LANES), bf16),
            pltpu.VMEM((pairs, 2 * rows, count * ff), bf16),
            pltpu.VMEM((pairs, rows, width), bf16),
            pltpu.VMEM((max(pairs - 1, 1), rows, width), bf16),
            dma((2, owners)), dma((2, owners)),
            dma((chips,)), dma((chips,)),
            dma((units, 2, dps)), dma((units, 2, dps)),
            dma((units,)), dma((units,)),
            dma((strips, 2, dps)), dma((strips, 2, dps)),
            dma((strips, dps)), dma((strips, dps)),
            dma((steps,)), dma((steps,)),
            dma((steps, pairs)), dma((steps, pairs)),
            dma((1,)), dma((units, 2)), dma((strips, local)), dma((steps,)),
        ],
        compiler_params=pltpu.CompilerParams(
            collective_id=0, has_side_effects=True, vmem_limit_bytes=67043328
        ),
    )(tokens, expert_ids.T, route_probs.T, w_gate_up, w_down)


def solution(mesh):
    return jax.shard_map(
        shards,
        mesh=mesh,
        in_specs=(
            P(("dp", "expert"), None),
            P(("dp", "expert"), None),
            P(("dp", "expert"), None),
            P("expert", "dp", None),
            P("expert", None, "dp"),
        ),
        out_specs=P(("dp", "expert"), None),
        check_vma=False,
    )
```

time: 250 us -> 208 us (0.83)
  Pallas kernels: 244 us -> 205 us
  other arithmetic: 5.47 us -> 0 us
    pallas_call x1, Pallas kernels: 244 us -> 205 us  [shards(): pl.pallas_call(functools.partial(kernel, dps, owners), out_shape=jax.Shap...]
    reduce_sum x3 -> x0, other arithmetic: 4.76 us -> none  [the longest x1 3.31 us: shards(): return jnp.sum(got.astype(jnp.float32), axis=0).astype(bf16)]
where the time goes in v1:
time: 208 us
  Pallas kernels  205 us (99%)
  local copies, waits for them, and re-layouts  2.3 us (1%)
    pallas_call x1, Pallas kernels, shards(): pl.pallas_call(functools.partial(kernel, dps, owners), out_shape=jax.Shap...  205 us

profile of v1, /device:TPU:0, one launch (start us, length us, event | category | flops | bytes accessed | tf_op | source)
XLA Modules:
  0.0 207.7 jit_solution(1495604435300499358)
XLA Ops:
  0.0 205.4 %shard_map.55 = bf16[256,2048]{1,0:T(8,128)(2,1)} custom-call(bf16[256,2048]{1,0:T(8,128)(2,1)} %tok_in.1, s32[8,256]{1,0:T(8,128)} %bitcast.2, f32[8,256]{1,0:T(8,128)} %bitcast.3, bf16[2,512,1536]{2,1,0:T(8,128)(2,1)} %gu_in.1, bf16[2,768,512]{2,1,0:T(8,128)(2,1)} %dn_in.1), custom_call_target="tpu_custom_call" | custom-call | tf_op jit(solution)/shard_map/pallas_call | solution.py:494
  205.4 2.3 %copy.7 = bf16[256,2048]{1,0:T(8,128)(2,1)} copy(bf16[256,2048]{1,0:T(8,128)(2,1)} %shard_map.55) | data formatting | bytes 2097152

commit v2 on v1

--- a/solution.py
+++ b/solution.py
@@ -54,12 +54,13 @@
             device_id_type=MESH,
         )
 
-    def own(self, stage):
-        for half, order in enumerate(self.orders):
-            self._copy(half, order[stage], 0).start()
-
-    def relay(self, stage):
-        for half, order in enumerate(self.orders):
+    def own(self, stage, halves=(0, 1)):
+        for half in halves:
+            self._copy(half, self.orders[half][stage], 0).start()
+
+    def relay(self, stage, halves=(0, 1)):
+        for half in halves:
+            order = self.orders[half]
             for s in span(order[:stage])[1:]:
                 self._copy(half, order[stage], s).start()
 
@@ -77,15 +78,16 @@
             device_id_type=MESH,
         ).wait_recv()
 
-    def wait(self, stage):
-        for half, order in enumerate(self.orders):
+    def wait(self, stage, halves=(0, 1)):
+        for half in halves:
+            order = self.orders[half]
             for s in span(order[:stage]):
                 self.take(half, order[stage] ^ s)
 
-    def forward(self):
+    def forward(self, halves=(0, 1)):
         for stage in range(1, self.last + 1):
-            self.wait(stage - 1)
-            self.relay(stage)
+            self.wait(stage - 1, halves)
+            self.relay(stage, halves)
 
     def drain(self):
         for half, order in enumerate(self.orders):
@@ -280,13 +282,15 @@
         def _():
             down_own(0)
 
-    begin, early = units // 3, 2 * units // 3
+    begin, early = 5 * units // 12, 2 * units // 3
 
     up(0).forward()
     for u in range(begin):
         relay_step(u, 2)
-        if u == begin // 2:
-            tokens.forward()
+        if u == 1:
+            tokens.forward((0,))
+        if u == 3:
+            tokens.forward((1,))
         up(u).wait(last)
         up_sib(u).start()
 
@@ -428,18 +432,18 @@
         if 0 <= k - 2 * lag < len(steps):
             finish(k - 2 * lag)
 
-    if strips > 1:
-        down_own(1)
+    def down_next(s):
+        if s < strips:
+            down(s).forward()
+        if s + 1 < strips:
+            down_own(s + 1)
+
     for s in range(strips):
         down_sib(s, dp, 0).wait_recv()
         advance(s)
         if s == 0:
-            down(0).forward()
-        if s == strips // 2:
-            if strips > 2:
-                down_own(2)
-            if strips > 1:
-                down(1).forward()
+            down_next(0)
+    down_next(1)
     k = strips
     for s in range(strips):
         down(s).wait(last)
@@ -449,11 +453,7 @@
             down_sib(s, xor(dp, m), m).wait_recv()
             advance(k)
             k += 1
-            if m == 1:
-                if s + 3 < strips:
-                    down_own(s + 3)
-                if s + 2 < strips:
-                    down(s + 2).forward()
+        down_next(s + 2)
     while k < len(steps) + 2 * lag:
         advance(k)
         k += 1

time: 208 us -> 203 us (0.976)
  Pallas kernels: 205 us -> 200 us
    pallas_call x1, Pallas kernels: 205 us -> 200 us  [shards(): pl.pallas_call(functools.partial(kernel, dps, owners), out_shape=jax.Shap...]
where the time goes in v2:
time: 203 us; the launch traced here: 202 us
  Pallas kernels  200 us (99%)
  local copies, waits for them, and re-layouts  2.3 us (1%)
    pallas_call x1, Pallas kernels, shards(): pl.pallas_call(functools.partial(kernel, dps, owners), out_shape=jax.Shap...  200 us

profile of v2, /device:TPU:0, one launch (start us, length us, event | category | flops | bytes accessed | tf_op | source)
XLA Modules:
  0.0 202.3 jit_solution(14716134592827899157)
XLA Ops:
  0.0 200.0 %shard_map.55 = bf16[256,2048]{1,0:T(8,128)(2,1)} custom-call(bf16[256,2048]{1,0:T(8,128)(2,1)} %tok_in.1, s32[8,256]{1,0:T(8,128)} %bitcast.2, f32[8,256]{1,0:T(8,128)} %bitcast.3, bf16[2,512,1536]{2,1,0:T(8,128)(2,1)} %gu_in.1, bf16[2,768,512]{2,1,0:T(8,128)(2,1)} %dn_in.1), custom_call_target="tpu_custom_call" | custom-call | tf_op jit(solution)/shard_map/pallas_call | solution.py:494
  200.0 2.3 %copy.7 = bf16[256,2048]{1,0:T(8,128)(2,1)} copy(bf16[256,2048]{1,0:T(8,128)(2,1)} %shard_map.55) | data formatting | bytes 2097152
